TPU v7x, 32 devices: a whole 2x2x4 slice. The times are simulated.
32 devices in a mesh: patch: 8 (over z, x), member: 4 (over y, core).
Axes of the slice: x: 2, y: 2, z: 4, core: 2. Of those that a mesh axis runs over, the one named last changes fastest.
Arguments:
- background: bfloat16 [32, 16, 3, 64, 128], P('patch', None, None, 'member'), may hold values from -6 to 6
- patch_blocks: int32 [32], replicated, may hold values from 1 to 16, as said below
- obs_values: float32 [16384], P(('patch', 'member')), may hold values from -12 to 12
- obs_errors: float32 [16384], P(('patch', 'member')), may hold values from 0.5 to 2
- obs_patch: int32 [16384], P('patch'), may hold values from 0 to 3
- obs_position: int32 [16384], P('patch'), may hold values from 0 to 1073741823
Outputs:
- analysis: bfloat16 [32, 16, 3, 64, 128], P('patch', None, None, 'member')
- inflation: float32 [], replicated
Inputs may be any that keep to these rules, and one draw needn't show every extreme that they name: `obs_patch`: index among the 4 patches held by the observation's index of patch. `patch_blocks`: the used blocks of the 4 patches of one index of patch sum to at most 32; some index reaches 32, and some patch uses all 16.
All inputs are finite; a program needn't handle non-finite values.
Results may differ from a plain program's by a relative error of at most 0.0065.
Values may be sent and summed in bfloat16 or wider, within the bound.
A program may use at most 64 MiB of HBM per device.

v0:
```python
import math
import jax
import jax.numpy as jnp
from jax import lax
from jax.sharding import PartitionSpec as P

K = 64
CB = 128
MAXB = 16
NS_STEPS = 4
PD = 4
OBS_DEV = 2048
neighbour_weight = 0.5


def extended(array, sides, width):
    for axis, dim in sides:
        count, length = (lax.axis_size(axis), array.shape[dim])
        up = [(i, (i + 1) % count) for i in range(count - 1)]
        down = [(j, i) for i, j in up]
        last = lax.slice_in_dim(array, length - width, length, axis=dim)
        initial = lax.slice_in_dim(array, 0, width, axis=dim)
        before = lax.ppermute(last, axis, up)
        after = lax.ppermute(initial, axis, down)
        array = jnp.concatenate([before, array, after], axis=dim)
    return array


def inverse_root(system):
    precise = lax.Precision.HIGHEST
    identity = jnp.eye(K, dtype=jnp.float32)
    norm_value = jnp.sqrt(jnp.sum(system * system, axis=(1, 2)))
    square_part = system / norm_value[:, None, None]
    inverse_part = jnp.broadcast_to(identity, system.shape)
    for sweep_index in range(NS_STEPS):
        middle = 1.5 * identity - 0.5 * jnp.einsum(
            "pij,pjk->pik", inverse_part, square_part, precision=precise
        )
        square_part = jnp.einsum("pij,pjk->pik", square_part, middle, precision=precise)
        inverse_part = jnp.einsum("pij,pjk->pik", middle, inverse_part, precision=precise)
    return inverse_part / jnp.sqrt(norm_value)[:, None, None]


def per_device(background, patch_blocks, obs_values, obs_errors, obs_patch, obs_position):
    precise = lax.Precision.HIGHEST
    member_count = lax.axis_size("member")
    local_members = K // member_count
    obs_share = OBS_DEV // member_count
    block_share = MAXB // member_count
    member_index = lax.axis_index("member")
    first_patch = lax.axis_index("patch") * PD
    used_blocks = lax.dynamic_slice_in_dim(patch_blocks, first_patch, PD)
    slot_table = jnp.arange(PD, dtype=jnp.int32)
    onehot_all = obs_patch[None, :] == slot_table[:, None]
    obs_counts = jnp.sum(jnp.where(onehot_all, used_blocks[:, None], 0), axis=0)
    cell_index = obs_position % (obs_counts * CB)
    flat_index = obs_patch * (MAXB * CB) + cell_index
    thickness = jnp.transpose(background[:, :, 0], (0, 1, 3, 2)).reshape(
        PD * MAXB * CB, local_members
    )
    sampled_local = thickness[flat_index]
    sampled = lax.all_to_all(sampled_local, "member", split_axis=0, concat_axis=1, tiled=True)
    own_slots = lax.dynamic_slice_in_dim(obs_patch, member_index * obs_share, obs_share)
    values = sampled.astype(jnp.float32)
    obs_mean = jnp.sum(values, axis=1) / K
    spread = values - obs_mean[:, None]
    innovation = obs_values - obs_mean
    variance = jnp.sum(spread * spread, axis=1) / (K - 1)
    misfit_part = jnp.sum(innovation * innovation)
    spread_part = jnp.sum(variance + obs_errors * obs_errors)
    weighted = spread / obs_errors[:, None]
    onehot = (own_slots[None, :] == slot_table[:, None]).astype(jnp.float32)
    masked = onehot[:, :, None] * weighted[None]
    gram_own = jnp.einsum("pjk,jl->pkl", masked, weighted, precision=precise)
    cross_own = jnp.einsum("pjk,j->pk", masked, innovation / obs_errors, precision=precise)
    stacked = jnp.concatenate([gram_own, cross_own[:, None, :]], axis=1)
    summed, misfit_member, spread_member = lax.psum((stacked, misfit_part, spread_part), "member")
    numerator, denominator = lax.psum((misfit_member, spread_member), "patch")
    inflation = numerator / denominator
    rimmed = extended(summed, (("patch", 0),), 1)
    localized = rimmed[1:-1] + neighbour_weight * (rimmed[:-2] + rimmed[2:])
    gram_local = localized[:, :K]
    cross_local = localized[:, K]
    identity = jnp.eye(K, dtype=jnp.float32)
    system = (K - 1) / inflation * identity + gram_local
    root_inverse = inverse_root(system)
    inner_weights = jnp.einsum("pkl,pl->pk", root_inverse, cross_local, precision=precise)
    mean_weights = jnp.einsum("pkl,pl->pk", root_inverse, inner_weights, precision=precise)
    transform = (mean_weights[:, :, None] + math.sqrt(K - 1) * root_inverse).astype(jnp.bfloat16)
    columns = lax.all_to_all(background, "member", split_axis=1, concat_axis=3, tiled=True)
    member_mean = jnp.sum(columns.astype(jnp.float32), axis=3) / K
    anomaly = (columns.astype(jnp.float32) - member_mean[:, :, :, None, :]).astype(jnp.bfloat16)
    combined = jnp.einsum(
        "pbvlc,plk->pbvkc", anomaly, transform, preferred_element_type=jnp.float32
    )
    block_ids = member_index * block_share + jnp.arange(block_share, dtype=jnp.int32)
    in_use = (block_ids[None, :] < used_blocks[:, None])[:, :, None, None, None]
    result = jnp.where(in_use, member_mean[:, :, :, None, :] + combined, 0.0).astype(jnp.bfloat16)
    analysis = lax.all_to_all(result, "member", split_axis=3, concat_axis=1, tiled=True)
    return (analysis, inflation)


def solution(mesh):
    in_specs = (
        P("patch", None, None, "member", None),
        P(),
        P(("patch", "member")),
        P(("patch", "member")),
        P("patch"),
        P("patch"),
    )
    out_specs = (P("patch", None, None, "member", None), P())
    return jax.shard_map(
        per_device, mesh=mesh, in_specs=in_specs, out_specs=out_specs, check_vma=False
    )
```

profile of v0, /device:TPU:0, one launch (start us, length us, event | category | flops | bytes accessed | tf_op | source)
XLA Modules:
  0.0 108.1 jit_solution(4150788410182912282)
XLA Ops:
  7.2 1.0 slice_bitcast_fusion
  8.2 1.0 copy.84
  9.6 6.2 %gather_fusion = bf16[2048,16]{1,0:T(8,128)(2,1)S(1)} fusion(bf16[8192,16]{1,0:T(8,128)(2,1)S(1)} %bitcast.75, s32[2048]{0:T(1024)S(1)} %fusion.30), kind=kCustom, calls=%fused_computation | custom fusion | bytes 139264 | tf_op jit(solution)/shard_map/gather | solution.py:61
  15.8 0.8 copy.85
  16.6 4.3 %all-to-all-start.1 = ((bf16[4,512,16]{1,2,0:T(8,128)(2,1)}), bf16[4,512,16]{1,2,0:T(8,128)(2,1)S(1)}, u32[]{:S(2)}, u32[]{:S(2)}) async-start(bf16[4,512,16]{1,2,0:T(8,128)(2,1)} %copy.85), calls=%async_computation.1 | async-start | bytes 131072 | tf_op jit(solution)/shard_map/all_to_all | solution.py:62
  21.0 1.0 copy.79
  22.0 2.9 %all-to-all-done.1 = bf16[4,512,16]{1,2,0:T(8,128)(2,1)S(1)} async-done(((bf16[4,512,16]{1,2,0:T(8,128)(2,1)}), bf16[4,512,16]{1,2,0:T(8,128)(2,1)S(1)}, u32[]{:S(2)}, u32[]{:S(2)}) %all-to-all-start.1) | async-done | bytes 65568 | tf_op jit(solution)/shard_map/all_to_all | solution.py:62
  25.0 3.5 %all-to-all-start = ((bf16[4,16,3,16,128]{4,3,2,0,1:T(8,128)(2,1)}), bf16[4,16,3,16,128]{4,3,2,0,1:T(8,128)(2,1)S(1)}, u32[]{:S(2)}, u32[]{:S(2)}) async-start(bf16[4,16,3,16,128]{4,3,2,0,1:T(8,128)(2,1)} %copy.79), calls=%async_computation | async-start | bytes 1572864 | tf_op jit(solution)/shard_map/all_to_all | solution.py:90
  28.6 0.7 multiply_reduce_fusion.2
  29.3 0.9 fusion.7
  30.2 0.6 convolution_bitcast_fusion
  30.7 0.8 pad_maximum_fusion.2
  31.7 10.3 %all-reduce.1 = (f32[]{:T(128)}, f32[]{:T(128)}) all-reduce(f32[]{:T(128)} %get-tuple-element.10, f32[]{:T(128)} %get-tuple-element.8), channel_id=1, replica_groups=mesh['patch'=8,'member'=4] {'member'}, use_global_device_ids=true, to_apply=%region_6.7 | all-reduce | flops 2 | bytes 16 | tf_op jit(solution)/shard_map/psum | solution.py:77
  42.0 22.8 %all-reduce = (f32[]{:T(128)}, f32[]{:T(128)}) all-reduce(f32[]{:T(128)} %get-tuple-element.4, f32[]{:T(128)} %get-tuple-element.5), channel_id=1, replica_groups=mesh['patch'=8,'member'=4] {'patch'}, use_global_device_ids=true, to_apply=%region_7.8 | all-reduce | flops 2 | bytes 16 | tf_op jit(solution)/shard_map/psum | solution.py:78
  66.2 0.8 fusion.36
  67.0 2.8 %collective-permute-start = (f32[1,65,64]{1,2,0:T(8,128)S(1)}, f32[1,65,64]{1,2,0:T(8,128)S(1)}, u32[]{:S(2)}, u32[]{:S(2)}) collective-permute-start(f32[1,65,64]{1,2,0:T(8,128)S(1)} %get-tuple-element.6), channel_id=1, source_target_pairs={{0,4},{4,8},{8,12},{12,16},{16,20},{20,24},{24,28},{1,5},{5,9},{9,... | collective-permute-start | bytes 49928 | tf_op jit(solution)/shard_map/ppermute | solution.py:23
  69.8 1.3 %collective-permute-start.1 = (f32[1,65,64]{1,2,0:T(8,128)S(1)}, f32[1,65,64]{1,2,0:T(8,128)S(1)}, u32[]{:S(2)}, u32[]{:S(2)}) collective-permute-start(f32[1,65,64]{1,2,0:T(8,128)S(1)} %get-tuple-element.7), channel_id=1, source_target_pairs={{4,0},{8,4},{12,8},{16,12},{20,16},{24,20},{28,24},{5,1},{9,5},{13... | collective-permute-start | bytes 49928 | tf_op jit(solution)/shard_map/ppermute | solution.py:24
  71.3 4.2 %collective-permute-done.1 = f32[1,65,64]{1,2,0:T(8,128)S(1)} collective-permute-done((f32[1,65,64]{1,2,0:T(8,128)S(1)}, f32[1,65,64]{1,2,0:T(8,128)S(1)}, u32[]{:S(2)}, u32[]{:S(2)}) %collective-permute-start.1) | collective-permute-done | bytes 16672 | tf_op jit(solution)/shard_map/ppermute | solution.py:24
  75.6 1.1 %fusion.15 = f32[4,65,64]{1,2,0:T(8,128)S(1)} fusion(f32[4,65,64]{1,2,0:T(8,128)} %all-reduce.4.cloned.1.call-done, f32[1,65,64]{1,2,0:T(8,128)S(1)} %collective-permute-done.1, f32[1,65,64]{1,2,0:T(8,128)S(1)} %collective-permute-done), kind=kLoop, calls=%fused_computation.30 | loop fusion | flops 83200 | bytes 166400 | tf_op jit(solution)/shard_map/add | solution.py:81
  81.9 0.5 fusion.1
  82.4 1.5 %copy.92 = bf16[4,4,3,64,128]{4,1,2,0,3:T(4,128)(2,1)} copy(bf16[4,4,3,64,128]{4,3,2,1,0:T(8,128)(2,1)S(1)} %fusion.1) | data formatting | bytes 1572864 | tf_op jit(solution)/shard_map/convert_element_type | solution.py:98
  83.9 3.5 %all-to-all-start.2 = ((bf16[4,4,3,64,128]{4,1,2,0,3:T(4,128)(2,1)}), bf16[4,4,3,64,128]{4,1,2,0,3:T(4,128)(2,1)S(1)}, u32[]{:S(2)}, u32[]{:S(2)}) async-start(bf16[4,4,3,64,128]{4,1,2,0,3:T(4,128)(2,1)} %copy.92), calls=%async_computation.2 | async-start | bytes 1572864 | tf_op jit(solution)/shard_map/all_to_all | solution.py:99
  88.7 10.3 %all-to-all-done.2 = bf16[4,4,3,64,128]{4,1,2,0,3:T(4,128)(2,1)S(1)} async-done(((bf16[4,4,3,64,128]{4,1,2,0,3:T(4,128)(2,1)}), bf16[4,4,3,64,128]{4,1,2,0,3:T(4,128)(2,1)S(1)}, u32[]{:S(2)}, u32[]{:S(2)}) %all-to-all-start.2) | async-done | bytes 786464 | tf_op jit(solution)/shard_map/all_to_all | solution.py:99
  99.0 1.1 %copy.93 = bf16[4,4,4,3,16,128]{5,4,3,2,1,0:T(8,128)(2,1)} copy(bf16[4,4,4,3,16,128]{5,2,3,0,4,1:T(4,128)(2,1)S(1)} %bitcast.77) | data formatting | bytes 1572864 | tf_op jit(solution)/shard_map/all_to_all | solution.py:99
  (56 shorter events, 6.3 us)
Async XLA Ops:
  7.2 2.1 %copy-start.5 = (s32[32]{0:T(128)S(1)}, s32[32]{0:T(128)}, u32[]{:S(2)}) copy-start(s32[32]{0:T(128)} %param.7) | copy-start | bytes 388
  7.2 2.1 %copy-start.1 = (s32[2048]{0:T(1024)S(1)}, s32[2048]{0:T(1024)}, u32[]{:S(2)}) copy-start(s32[2048]{0:T(1024)} %param.10) | copy-start | bytes 24580
  7.2 2.2 %copy-start.3 = (s32[2048]{0:T(1024)S(1)}, s32[2048]{0:T(1024)}, u32[]{:S(2)}) copy-start(s32[2048]{0:T(1024)} %param.11) | copy-start | bytes 24580
  9.6 11.4 %copy-start = (bf16[4,16,3,16,128]{4,3,2,1,0:T(8,128)(2,1)S(1)}, bf16[4,16,3,16,128]{4,3,2,1,0:T(8,128)(2,1)}, u32[]{:S(2)}) copy-start(bf16[4,16,3,16,128]{4,3,2,1,0:T(8,128)(2,1)} %param.6) | copy-start | bytes 2359300
  16.6 8.4 %all-to-all-start.1 = ((bf16[4,512,16]{1,2,0:T(8,128)(2,1)}), bf16[4,512,16]{1,2,0:T(8,128)(2,1)S(1)}, u32[]{:S(2)}, u32[]{:S(2)}) async-start(bf16[4,512,16]{1,2,0:T(8,128)(2,1)} %copy.85), calls=%async_computation.1 | async-start | bytes 131072 | tf_op jit(solution)/shard_map/all_to_all | solution.py:62
  21.0 7.6 %copy-start.2 = (f32[512]{0:T(512)S(1)}, f32[512]{0:T(512)}, u32[]{:S(2)}) copy-start(f32[512]{0:T(512)} %param.9) | copy-start | bytes 6148
  21.0 7.6 %copy-start.4 = (f32[512]{0:T(512)S(1)}, f32[512]{0:T(512)}, u32[]{:S(2)}) copy-start(f32[512]{0:T(512)} %param.8) | copy-start | bytes 6148
  25.0 55.9 %all-to-all-start = ((bf16[4,16,3,16,128]{4,3,2,0,1:T(8,128)(2,1)}), bf16[4,16,3,16,128]{4,3,2,0,1:T(8,128)(2,1)S(1)}, u32[]{:S(2)}, u32[]{:S(2)}) async-start(bf16[4,16,3,16,128]{4,3,2,0,1:T(8,128)(2,1)} %copy.79), calls=%async_computation | async-start | bytes 1572864 | tf_op jit(solution)/shard_map/all_to_all | solution.py:90
  28.5 37.7 %all-reduce.4.cloned.1.call-start = ((), (), s32[]{:S(2)}) async-start(), calls=%async_computation.3 | async-start | bytes 262144 | tf_op jit(solution)/shard_map/psum | solution.py:77
  67.0 4.4 %collective-permute-start = (f32[1,65,64]{1,2,0:T(8,128)S(1)}, f32[1,65,64]{1,2,0:T(8,128)S(1)}, u32[]{:S(2)}, u32[]{:S(2)}) collective-permute-start(f32[1,65,64]{1,2,0:T(8,128)S(1)} %get-tuple-element.6), channel_id=1, source_target_pairs={{0,4},{4,8},{8,12},{12,16},{16,20},{20,24},{24,28},{1,5},{5,9},{9,... | collective-permute-start | bytes 49928 | tf_op jit(solution)/shard_map/ppermute | solution.py:23
  69.8 5.8 %collective-permute-start.1 = (f32[1,65,64]{1,2,0:T(8,128)S(1)}, f32[1,65,64]{1,2,0:T(8,128)S(1)}, u32[]{:S(2)}, u32[]{:S(2)}) collective-permute-start(f32[1,65,64]{1,2,0:T(8,128)S(1)} %get-tuple-element.7), channel_id=1, source_target_pairs={{4,0},{8,4},{12,8},{16,12},{20,16},{24,20},{28,24},{5,1},{9,5},{13... | collective-permute-start | bytes 49928 | tf_op jit(solution)/shard_map/ppermute | solution.py:24
  83.9 15.1 %all-to-all-start.2 = ((bf16[4,4,3,64,128]{4,1,2,0,3:T(4,128)(2,1)}), bf16[4,4,3,64,128]{4,1,2,0,3:T(4,128)(2,1)S(1)}, u32[]{:S(2)}, u32[]{:S(2)}) async-start(bf16[4,4,3,64,128]{4,1,2,0,3:T(4,128)(2,1)} %copy.92), calls=%async_computation.2 | async-start | bytes 1572864 | tf_op jit(solution)/shard_map/all_to_all | solution.py:99
Sparse Core Ops, SparseCore 0:
  31.6 33.9 all-reduce.3
where the time goes:
time: 109 us; the launch traced here: 108 us
  blocking collectives  33.1 us (30%)
  between operations  18.1 us (17%)
  waiting for transfers between devices  17.7 us (16%)
  starting transfers between devices  15.4 us (14%)
  local copies, waits for them, and re-layouts  14.1 us (13%)
  matrix products  5.75 us (5%)
  other arithmetic  3.89 us (4%)
    psum x1, blocking collectives, per_device(): numerator, denominator = lax.psum((misfit_member, spread_member), 'patch')  22.8 us
    psum x1, blocking collectives, per_device(): lax.psum((stacked, misfit_part, spread_part), 'member')  10.3 us
    all_to_all x1, waiting for transfers between devices, per_device(): lax.all_to_all(result, 'member', split_axis=3, concat_axis=1, tiled=True)  10.3 us
    gather x1, local copies, waits for them, and re-layouts, per_device(): sampled_local = thickness[flat_index]  6.18 us
    all_to_all x1, starting transfers between devices, per_device(): lax.all_to_all(sampled_local, 'member', split_axis=0, concat_axis=1, tile...  4.26 us
    ppermute x1, waiting for transfers between devices, extended(): after = lax.ppermute(initial, axis, down)  4.23 us
    all_to_all x1, starting transfers between devices, per_device(): lax.all_to_all(background, 'member', split_axis=1, concat_axis=3, tiled=T...  3.49 us
    all_to_all x1, starting transfers between devices, per_device(): lax.all_to_all(result, 'member', split_axis=3, concat_axis=1, tiled=True)  3.49 us
  transfers between devices with their start and end apart: 6, of which 4 were waited for; matrix products, arithmetic and copies ran while one was open for 10% of the time, Pallas kernels for 0%

commit v1 on v0

--- a/solution.py
+++ b/solution.py
@@ -11,6 +11,22 @@
 PD = 4
 OBS_DEV = 2048
 neighbour_weight = 0.5
+
+
+def swapped_with_each(shard, axis, split, join):
+    ways, here = (lax.axis_size(axis), lax.axis_index(axis))
+    width = shard.shape[split] // ways
+    lengths = list(shard.shape)
+    lengths[split] = width
+    height = lengths[join]
+    lengths[join] = height * ways
+    full = jnp.zeros(lengths, shard.dtype)
+    for mask in range(ways):
+        part = lax.dynamic_slice_in_dim(shard, (here ^ mask) * width, width, axis=split)
+        if mask:
+            part = lax.ppermute(part, axis, [(d, d ^ mask) for d in range(ways)])
+        full = lax.dynamic_update_slice_in_dim(full, part, (here ^ mask) * height, axis=join)
+    return full
 
 
 def extended(array, sides, width):
@@ -96,7 +112,7 @@
     block_ids = member_index * block_share + jnp.arange(block_share, dtype=jnp.int32)
     in_use = (block_ids[None, :] < used_blocks[:, None])[:, :, None, None, None]
     result = jnp.where(in_use, member_mean[:, :, :, None, :] + combined, 0.0).astype(jnp.bfloat16)
-    analysis = lax.all_to_all(result, "member", split_axis=3, concat_axis=1, tiled=True)
+    analysis = swapped_with_each(result, "member", 3, 1)
     return (analysis, inflation)
 
 

time: 109 us -> 104 us (0.954)
  starting transfers between devices: 15.4 us -> 13.8 us
  waiting for transfers between devices: 17.7 us -> 16.4 us
  local copies, waits for them, and re-layouts: 14.1 us -> 12.8 us
    all_to_all x1 -> x0, waiting for transfers between devices: 10.3 us -> none  [per_device(): lax.all_to_all(result, 'member', split_axis=3, concat_axis=1, tiled=True)]
    ppermute x0 -> x3, waiting for transfers between devices: none -> 8.93 us  [swapped_with_each(): part = lax.ppermute(part, axis, [(d, d ^ mask) for d in range(ways)])]
    all_to_all x1 -> x0, starting transfers between devices: 3.49 us -> none  [per_device(): lax.all_to_all(result, 'member', split_axis=3, concat_axis=1, tiled=True)]
    ppermute x0 -> x3, starting transfers between devices: none -> 1.97 us  [swapped_with_each(): part = lax.ppermute(part, axis, [(d, d ^ mask) for d in range(ways)])]
    convert_element_type x1 -> x0, local copies, waits for them, and re-layouts: 1.49 us -> none  [per_device(): jnp.where(in_use, member_mean[:, :, :, None, :] + combined, 0.0)]
  transfers between devices with their start and end apart: 6 -> 8, of which waited for: 4 -> 5; matrix products, arithmetic and copies ran while one was open for 10% -> 10% of each run, Pallas kernels for 0% -> 0%
where the time goes in v1:
time: 104 us
  blocking collectives  33.1 us (32%)
  between operations  18.2 us (18%)
  waiting for transfers between devices  16.4 us (16%)
  starting transfers between devices  13.8 us (13%)
  local copies, waits for them, and re-layouts  12.8 us (12%)
  matrix products  5.74 us (6%)
  other arithmetic  3.9 us (4%)
    psum x1, blocking collectives, per_device(): numerator, denominator = lax.psum((misfit_member, spread_member), 'patch')  22.8 us
    psum x1, blocking collectives, per_device(): lax.psum((stacked, misfit_part, spread_part), 'member')  10.3 us
    ppermute x3, waiting for transfers between devices, swapped_with_each(): part = lax.ppermute(part, axis, [(d, d ^ mask) for d in range(ways)])  8.93 us
    gather x1, local copies, waits for them, and re-layouts, per_device(): sampled_local = thickness[flat_index]  6.18 us
    all_to_all x1, starting transfers between devices, per_device(): lax.all_to_all(sampled_local, 'member', split_axis=0, concat_axis=1, tile...  4.26 us
    ppermute x1, waiting for transfers between devices, extended(): after = lax.ppermute(initial, axis, down)  4.23 us
    all_to_all x1, starting transfers between devices, per_device(): lax.all_to_all(background, 'member', split_axis=1, concat_axis=3, tiled=T...  3.49 us
    all_to_all x1, waiting for transfers between devices, per_device(): lax.all_to_all(sampled_local, 'member', split_axis=0, concat_axis=1, tile...  2.91 us
  transfers between devices with their start and end apart: 8, of which 5 were waited for; matrix products, arithmetic and copies ran while one was open for 10% of the time, Pallas kernels for 0%

profile of v1, /device:TPU:0, one launch (start us, length us, event | category | flops | bytes accessed | tf_op | source)
XLA Modules:
  0.0 104.0 jit_solution(3360559319683197288)
XLA Ops:
  7.2 1.0 slice_bitcast_fusion
  8.2 1.0 copy.74
  9.6 6.2 %gather_fusion = bf16[2048,16]{1,0:T(8,128)(2,1)S(1)} fusion(bf16[8192,16]{1,0:T(8,128)(2,1)S(1)} %bitcast.77, s32[2048]{0:T(1024)S(1)} %fusion.29), kind=kCustom, calls=%fused_computation | custom fusion | bytes 139264 | tf_op jit(solution)/shard_map/gather | solution.py:77
  15.8 0.8 copy.75
  16.6 4.3 %all-to-all-start.1 = ((bf16[4,512,16]{1,2,0:T(8,128)(2,1)}), bf16[4,512,16]{1,2,0:T(8,128)(2,1)S(1)}, u32[]{:S(2)}, u32[]{:S(2)}) async-start(bf16[4,512,16]{1,2,0:T(8,128)(2,1)} %copy.75), calls=%async_computation.1 | async-start | bytes 131072 | tf_op jit(solution)/shard_map/all_to_all | solution.py:78
  21.0 1.0 copy.69
  22.0 2.9 %all-to-all-done.1 = bf16[4,512,16]{1,2,0:T(8,128)(2,1)S(1)} async-done(((bf16[4,512,16]{1,2,0:T(8,128)(2,1)}), bf16[4,512,16]{1,2,0:T(8,128)(2,1)S(1)}, u32[]{:S(2)}, u32[]{:S(2)}) %all-to-all-start.1) | async-done | bytes 65568 | tf_op jit(solution)/shard_map/all_to_all | solution.py:78
  25.0 3.5 %all-to-all-start = ((bf16[4,16,3,16,128]{4,3,2,0,1:T(8,128)(2,1)}), bf16[4,16,3,16,128]{4,3,2,0,1:T(8,128)(2,1)S(1)}, u32[]{:S(2)}, u32[]{:S(2)}) async-start(bf16[4,16,3,16,128]{4,3,2,0,1:T(8,128)(2,1)} %copy.69), calls=%async_computation | async-start | bytes 1572864 | tf_op jit(solution)/shard_map/all_to_all | solution.py:106
  28.6 0.7 multiply_reduce_fusion.2
  29.3 0.9 fusion.6
  30.2 0.5 convolution_bitcast_fusion
  30.7 0.8 pad_maximum_fusion.2
  31.7 10.3 %all-reduce.1 = (f32[]{:T(128)}, f32[]{:T(128)}) all-reduce(f32[]{:T(128)} %get-tuple-element.13, f32[]{:T(128)} %get-tuple-element.11), channel_id=1, replica_groups=mesh['patch'=8,'member'=4] {'member'}, use_global_device_ids=true, to_apply=%region_6.7 | all-reduce | flops 2 | bytes 16 | tf_op jit(solution)/shard_map/psum | solution.py:93
  42.0 22.8 %all-reduce = (f32[]{:T(128)}, f32[]{:T(128)}) all-reduce(f32[]{:T(128)} %get-tuple-element.4, f32[]{:T(128)} %get-tuple-element.5), channel_id=1, replica_groups=mesh['patch'=8,'member'=4] {'patch'}, use_global_device_ids=true, to_apply=%region_7.8 | all-reduce | flops 2 | bytes 16 | tf_op jit(solution)/shard_map/psum | solution.py:94
  66.2 0.8 fusion.35
  67.0 2.8 %collective-permute-start = (f32[1,65,64]{1,2,0:T(8,128)S(1)}, f32[1,65,64]{1,2,0:T(8,128)S(1)}, u32[]{:S(2)}, u32[]{:S(2)}) collective-permute-start(f32[1,65,64]{1,2,0:T(8,128)S(1)} %get-tuple-element.9), channel_id=1, source_target_pairs={{0,4},{4,8},{8,12},{12,16},{16,20},{20,24},{24,28},{1,5},{5,9},{9,... | collective-permute-start | bytes 49928 | tf_op jit(solution)/shard_map/ppermute | solution.py:39
  69.7 1.3 %collective-permute-start.1 = (f32[1,65,64]{1,2,0:T(8,128)S(1)}, f32[1,65,64]{1,2,0:T(8,128)S(1)}, u32[]{:S(2)}, u32[]{:S(2)}) collective-permute-start(f32[1,65,64]{1,2,0:T(8,128)S(1)} %get-tuple-element.10), channel_id=1, source_target_pairs={{4,0},{8,4},{12,8},{16,12},{20,16},{24,20},{28,24},{5,1},{9,5},{13... | collective-permute-start | bytes 49928 | tf_op jit(solution)/shard_map/ppermute | solution.py:40
  71.3 4.2 %collective-permute-done.1 = f32[1,65,64]{1,2,0:T(8,128)S(1)} collective-permute-done((f32[1,65,64]{1,2,0:T(8,128)S(1)}, f32[1,65,64]{1,2,0:T(8,128)S(1)}, u32[]{:S(2)}, u32[]{:S(2)}) %collective-permute-start.1) | collective-permute-done | bytes 16672 | tf_op jit(solution)/shard_map/ppermute | solution.py:40
  75.6 1.1 %fusion.14 = f32[4,65,64]{1,2,0:T(8,128)S(1)} fusion(f32[4,65,64]{1,2,0:T(8,128)} %all-reduce.4.cloned.1.call-done, f32[1,65,64]{1,2,0:T(8,128)S(1)} %collective-permute-done.1, f32[1,65,64]{1,2,0:T(8,128)S(1)} %collective-permute-done), kind=kLoop, calls=%fused_computation.33 | loop fusion | flops 83200 | bytes 166400 | tf_op jit(solution)/shard_map/add | solution.py:97
  84.0 0.6 collective-permute-start.3
  84.6 1.3 %collective-permute-start.4 = (bf16[4,4,3,16,128]{4,3,2,1,0:T(8,128)(2,1)S(1)}, bf16[4,4,3,16,128]{4,3,2,1,0:T(8,128)(2,1)S(1)}, u32[]{:S(2)}, u32[]{:S(2)}) collective-permute-start(bf16[4,4,3,16,128]{4,3,2,1,0:T(8,128)(2,1)S(1)} %get-tuple-element.6), channel_id=1, source_target_pairs={{0,3},{1,2},{2,1},{3,0},{4,7},{5,6},{6,5},{7,4},{8,11},{9,10},{10,... | collective-permute-start | bytes 589832 | tf_op jit(solution)/shard_map/ppermute | solution.py:27
  86.1 5.7 %collective-permute-done.3 = bf16[4,4,3,16,128]{4,3,2,1,0:T(8,128)(2,1)S(1)} collective-permute-done((bf16[4,4,3,16,128]{4,3,2,1,0:T(8,128)(2,1)S(1)}, bf16[4,4,3,16,128]{4,3,2,1,0:T(8,128)(2,1)S(1)}, u32[]{:S(2)}, u32[]{:S(2)}) %collective-permute-start.3) | collective-permute-done | bytes 196640 | tf_op jit(solution)/shard_map/ppermute | solution.py:27
  91.9 3.2 %collective-permute-done.4 = bf16[4,4,3,16,128]{4,3,2,1,0:T(8,128)(2,1)S(1)} collective-permute-done((bf16[4,4,3,16,128]{4,3,2,1,0:T(8,128)(2,1)S(1)}, bf16[4,4,3,16,128]{4,3,2,1,0:T(8,128)(2,1)S(1)}, u32[]{:S(2)}, u32[]{:S(2)}) %collective-permute-start.4) | collective-permute-done | bytes 196640 | tf_op jit(solution)/shard_map/ppermute | solution.py:27
  95.1 0.9 copy-done.1
  (66 shorter events, 7.2 us)
Async XLA Ops:
  7.2 2.1 %copy-start.6 = (s32[32]{0:T(128)S(1)}, s32[32]{0:T(128)}, u32[]{:S(2)}) copy-start(s32[32]{0:T(128)} %param.7) | copy-start | bytes 388
  7.2 2.1 %copy-start.2 = (s32[2048]{0:T(1024)S(1)}, s32[2048]{0:T(1024)}, u32[]{:S(2)}) copy-start(s32[2048]{0:T(1024)} %param.10) | copy-start | bytes 24580
  7.2 2.2 %copy-start.4 = (s32[2048]{0:T(1024)S(1)}, s32[2048]{0:T(1024)}, u32[]{:S(2)}) copy-start(s32[2048]{0:T(1024)} %param.11) | copy-start | bytes 24580
  9.6 11.4 %copy-start = (bf16[4,16,3,16,128]{4,3,2,1,0:T(8,128)(2,1)S(1)}, bf16[4,16,3,16,128]{4,3,2,1,0:T(8,128)(2,1)}, u32[]{:S(2)}) copy-start(bf16[4,16,3,16,128]{4,3,2,1,0:T(8,128)(2,1)} %param.6) | copy-start | bytes 2359300
  16.6 8.4 %all-to-all-start.1 = ((bf16[4,512,16]{1,2,0:T(8,128)(2,1)}), bf16[4,512,16]{1,2,0:T(8,128)(2,1)S(1)}, u32[]{:S(2)}, u32[]{:S(2)}) async-start(bf16[4,512,16]{1,2,0:T(8,128)(2,1)} %copy.75), calls=%async_computation.1 | async-start | bytes 131072 | tf_op jit(solution)/shard_map/all_to_all | solution.py:78
  21.0 7.6 %copy-start.3 = (f32[512]{0:T(512)S(1)}, f32[512]{0:T(512)}, u32[]{:S(2)}) copy-start(f32[512]{0:T(512)} %param.9) | copy-start | bytes 6148
  21.0 7.6 %copy-start.5 = (f32[512]{0:T(512)S(1)}, f32[512]{0:T(512)}, u32[]{:S(2)}) copy-start(f32[512]{0:T(512)} %param.8) | copy-start | bytes 6148
  25.0 55.9 %all-to-all-start = ((bf16[4,16,3,16,128]{4,3,2,0,1:T(8,128)(2,1)}), bf16[4,16,3,16,128]{4,3,2,0,1:T(8,128)(2,1)S(1)}, u32[]{:S(2)}, u32[]{:S(2)}) async-start(bf16[4,16,3,16,128]{4,3,2,0,1:T(8,128)(2,1)} %copy.69), calls=%async_computation | async-start | bytes 1572864 | tf_op jit(solution)/shard_map/all_to_all | solution.py:106
  28.5 37.7 %all-reduce.4.cloned.1.call-start = ((), (), s32[]{:S(2)}) async-start(), calls=%async_computation.2 | async-start | bytes 262144 | tf_op jit(solution)/shard_map/psum | solution.py:93
  67.0 4.4 %collective-permute-start = (f32[1,65,64]{1,2,0:T(8,128)S(1)}, f32[1,65,64]{1,2,0:T(8,128)S(1)}, u32[]{:S(2)}, u32[]{:S(2)}) collective-permute-start(f32[1,65,64]{1,2,0:T(8,128)S(1)} %get-tuple-element.9), channel_id=1, source_target_pairs={{0,4},{4,8},{8,12},{12,16},{16,20},{20,24},{24,28},{1,5},{5,9},{9,... | collective-permute-start | bytes 49928 | tf_op jit(solution)/shard_map/ppermute | solution.py:39
  69.7 5.8 %collective-permute-start.1 = (f32[1,65,64]{1,2,0:T(8,128)S(1)}, f32[1,65,64]{1,2,0:T(8,128)S(1)}, u32[]{:S(2)}, u32[]{:S(2)}) collective-permute-start(f32[1,65,64]{1,2,0:T(8,128)S(1)} %get-tuple-element.10), channel_id=1, source_target_pairs={{4,0},{8,4},{12,8},{16,12},{20,16},{24,20},{28,24},{5,1},{9,5},{13... | collective-permute-start | bytes 49928 | tf_op jit(solution)/shard_map/ppermute | solution.py:40
  82.6 3.5 %collective-permute-start.2 = (bf16[4,4,3,16,128]{4,3,2,1,0:T(8,128)(2,1)S(1)}, bf16[4,4,3,16,128]{4,3,2,1,0:T(8,128)(2,1)S(1)}, u32[]{:S(2)}, u32[]{:S(2)}) collective-permute-start(bf16[4,4,3,16,128]{4,3,2,1,0:T(8,128)(2,1)S(1)} %get-tuple-element.8), channel_id=1, source_target_pairs={{0,1},{1,0},{2,3},{3,2},{4,5},{5,4},{6,7},{7,6},{8,9},{9,8},{10,11... | collective-permute-start | bytes 589832 | tf_op jit(solution)/shard_map/ppermute | solution.py:27
  84.0 7.8 %collective-permute-start.3 = (bf16[4,4,3,16,128]{4,3,2,1,0:T(8,128)(2,1)S(1)}, bf16[4,4,3,16,128]{4,3,2,1,0:T(8,128)(2,1)S(1)}, u32[]{:S(2)}, u32[]{:S(2)}) collective-permute-start(bf16[4,4,3,16,128]{4,3,2,1,0:T(8,128)(2,1)S(1)} %get-tuple-element.7), channel_id=1, source_target_pairs={{0,2},{1,3},{2,0},{3,1},{4,6},{5,7},{6,4},{7,5},{8,10},{9,11},{10,... | collective-permute-start | bytes 589832 | tf_op jit(solution)/shard_map/ppermute | solution.py:27
  84.6 10.5 %collective-permute-start.4 = (bf16[4,4,3,16,128]{4,3,2,1,0:T(8,128)(2,1)S(1)}, bf16[4,4,3,16,128]{4,3,2,1,0:T(8,128)(2,1)S(1)}, u32[]{:S(2)}, u32[]{:S(2)}) collective-permute-start(bf16[4,4,3,16,128]{4,3,2,1,0:T(8,128)(2,1)S(1)} %get-tuple-element.6), channel_id=1, source_target_pairs={{0,3},{1,2},{2,1},{3,0},{4,7},{5,6},{6,5},{7,4},{8,11},{9,10},{10,... | collective-permute-start | bytes 589832 | tf_op jit(solution)/shard_map/ppermute | solution.py:27
  95.1 0.9 copy-start.1
Sparse Core Ops, SparseCore 0:
  31.6 33.9 all-reduce.3
